TPU v7x, 32 devices: a whole 2x2x4 slice. The times are simulated.
32 devices in a mesh: hot: 8 (over z, y), cold: 4 (over x, core).
Axes of the slice: x: 2, y: 2, z: 4, core: 2. Of those that a mesh axis runs over, the one named last changes fastest.
Arguments:
- tokens: bfloat16 [64, 8192], replicated, may hold values from -6 to 6
- norm_gain: float32 [8192], replicated, may hold values from 0.1 to 1.9
- hot_gate: bfloat16 [512, 8192], P(('hot', 'cold')), may hold values from -0.0625 to 0.0625
- hot_up: bfloat16 [512, 8192], P(('hot', 'cold')), may hold values from -0.0625 to 0.0625
- hot_down: bfloat16 [512, 8192], P(('hot', 'cold')), may hold values from -0.09375 to 0.09375
- hot_index: int32 [512], replicated, may hold values from 0 to 14335, as said below
- cold_gate: bfloat16 [8192, 14336], P('hot', 'cold'), may hold values from -0.0625 to 0.0625
- cold_up: bfloat16 [8192, 14336], P('hot', 'cold'), may hold values from -0.0625 to 0.0625
- cold_down: bfloat16 [14336, 8192], P('cold', 'hot'), may hold values from -0.0625 to 0.0625
- block_mask: int32 [64, 112], P(None, 'cold'), may hold values from 0 to 1, as said below
Outputs:
- ffn_out: bfloat16 [64, 8192], P(None, ('hot', 'cold'))
Inputs may be any that keep to these rules, and one draw needn't show every extreme that they name: `hot_index`: distinct hidden units. `block_mask`: in each run of 28 blocks held by one index of cold, at most 14 blocks are active for any sequence, and some index reaches exactly 14.
All inputs are finite; a program needn't handle non-finite values.
Results may differ from a plain program's by a relative error of at most 0.0065.
Values may be sent and summed in bfloat16 or wider, within the bound.
No kernel may reach another device: no remote copies, remote signals or barrier semaphores. Data moves between devices by JAX's collectives and lax.ppermute only.
A program may use at most 64 MiB of HBM per device.

v0:
```python
import jax
import jax.numpy as jnp
from jax import lax
from jax.sharding import PartitionSpec as P

UNITS = 14336


def on_device(
    tokens,
    norm_gain,
    hot_gate,
    hot_up,
    hot_down,
    hot_index,
    cold_gate,
    cold_up,
    cold_down,
    block_mask,
):
    values = tokens.astype(jnp.float32)
    scale = lax.rsqrt(jnp.mean(values * values, axis=1, keepdims=True) + 1e-05)
    normed = (values * scale * norm_gain[None, :]).astype(jnp.bfloat16)
    dims = (((1,), (1,)), ((), ()))
    gate_hot = lax.dot_general(normed, hot_gate, dims, preferred_element_type=jnp.float32)
    up_hot = lax.dot_general(normed, hot_up, dims, preferred_element_type=jnp.float32)
    hidden_hot = (jax.nn.silu(gate_hot) * up_hot).astype(jnp.bfloat16)
    feat_rows = cold_gate.shape[0]
    unit_count = cold_gate.shape[1]
    blocks_here = block_mask.shape[1]
    block = unit_count // blocks_here
    seqs = tokens.shape[0]
    is_hot = jnp.zeros((UNITS,), jnp.float32).at[hot_index].set(1.0)
    local_hot = lax.dynamic_slice_in_dim(is_hot, lax.axis_index("cold") * unit_count, unit_count)
    normed_part = lax.dynamic_slice_in_dim(normed, lax.axis_index("hot") * feat_rows, feat_rows, 1)
    gate_w, up_w, down_w = (cold_gate, cold_up, cold_down)
    seq_live = block_mask.astype(jnp.float32)
    unit_live = (1.0 - local_hot).reshape(blocks_here, block)
    live = (seq_live[:, :, None] * unit_live[None, :, :]).reshape(seqs, unit_count)
    gate_part = jnp.dot(normed_part, gate_w, preferred_element_type=jnp.float32)
    up_part = jnp.dot(normed_part, up_w, preferred_element_type=jnp.float32)
    gate_cold, up_cold = lax.psum((gate_part, up_part), "hot")
    hidden_cold = (jax.nn.silu(gate_cold) * up_cold * live).astype(jnp.bfloat16)
    out_cold = jnp.dot(hidden_cold, down_w, preferred_element_type=jnp.float32)
    down_cols = lax.all_to_all(hot_down, ("hot", "cold"), split_axis=1, concat_axis=0, tiled=True)
    hidden_all = lax.all_gather(hidden_hot, ("hot", "cold"), axis=1, tiled=True)
    hot_total = jnp.dot(hidden_all, down_cols, preferred_element_type=jnp.float32)
    cold_total = lax.psum_scatter(out_cold, "cold", scatter_dimension=1, tiled=True)
    total = hot_total + cold_total
    return total.astype(jnp.bfloat16)


def solution(mesh):
    in_specs = (
        P(),
        P(),
        P(("hot", "cold"), None),
        P(("hot", "cold"), None),
        P(("hot", "cold"), None),
        P(),
        P("hot", "cold"),
        P("hot", "cold"),
        P("cold", "hot"),
        P(None, "cold"),
    )
    out_specs = P(None, ("hot", "cold"))
    return jax.shard_map(
        on_device, mesh=mesh, in_specs=in_specs, out_specs=out_specs, check_vma=False
    )
```

profile of v0, /device:TPU:0, one launch (start us, length us, event | category | flops | bytes accessed | tf_op | source)
XLA Modules:
  0.0 177.9 jit_solution(3256755410243305480)
XLA Ops:
  6.5 0.0 copy-start
  6.5 0.0 all-reduce.3.cloned.1.call-start
  6.5 1.6 fusion
  8.1 0.0 slice-start
  8.1 1.7 fusion.2
  9.8 0.0 slice-start.1
  9.8 5.6 %fusion.11 = f32[64,3584]{1,0:T(8,128)} fusion(bf16[1024,3584]{1,0:T(8,128)(2,1)} %param.17, bf16[64,8192]{1,0:T(8,128)(2,1)S(1)} %fusion.2, s32[]{:T(128)S(6)} %select_n.9), kind=kOutput, calls=%fused_computation.17 | convolution fusion | flops 469762048 | bytes 8388612 | tf_op jit(solution)/shard_map/dot_general | solution.py:41
  15.4 0.0 slice-done
  15.4 0.0 slice-done.1
  15.4 0.0 copy-start.3
  15.5 0.0 copy-start.4
  15.5 2.3 %fusion.13 = f32[64,3584]{1,0:T(8,128)} fusion(bf16[1024,3584]{1,0:T(8,128)(2,1)S(1)} %bitcast.25, bf16[64,8192]{1,0:T(8,128)(2,1)S(1)} %fusion.2, s32[]{:T(128)S(6)} %select_n.9), kind=kOutput, calls=%fused_computation.19 | convolution fusion | flops 469762048 | bytes 8388612 | tf_op jit(solution)/shard_map/dot_general | solution.py:40
  17.8 0.0 all-reduce.3.cloned.1.call-update
  17.8 0.0 copy-start.1
  17.8 0.0 copy-done.2
  17.8 0.7 copy.22
  18.5 7.3 %all-to-all-start = ((bf16[16,32,256]{2,0,1:T(8,128)(2,1)}), bf16[16,32,256]{2,0,1:T(8,128)(2,1)S(1)}, u32[]{:S(2)}, u32[]{:S(2)}) async-start(bf16[16,32,256]{2,0,1:T(8,128)(2,1)} %bitcast.23), calls=%async_computation | async-start | bytes 524288 | tf_op jit(solution)/shard_map/all_to_all | solution.py:45
  25.9 0.0 reduce-scatter.2.cloned.1.call-start
  25.9 0.0 copy-done.3
  26.0 0.1 copy.16
  26.0 0.0 copy-done.4
  26.1 2.5 %scatter_custom_fusion = f32[14336]{0:T(1024)S(1)} fusion(s32[512]{0:T(512)S(1)} %compare_select_fusion, f32[512]{0:T(512)S(1)} %broadcast.20, f32[]{:T(128)} %constant.12.clone.1), kind=kCustom, calls=%fused_computation.21 | custom fusion | bytes 57348 | tf_op jit(solution)/shard_map/scatter | solution.py:33
  28.6 0.1 dynamic-slice_subtract_fusion
  28.6 93.3 %all-reduce.3.cloned.1.call-done = (f32[64,3584]{1,0:T(8,128)}, f32[64,3584]{1,0:T(8,128)}) async-done(((f32[64,3584]{1,0:T(8,128)}, f32[64,3584]{1,0:T(8,128)}), (f32[64,3584]{1,0:T(8,128)}, f32[64,3584]{1,0:T(8,128)})) %all-reduce.3.cloned.1.call-update) | async-done | bytes 1835024 | tf_op jit(solution)/shard_map/psum | solution.py:42
  121.9 0.3 mul.68
  122.3 6.2 %fusion.7 = f32[64,1024]{1,0:T(8,128)} fusion(bf16[3584,1024]{1,0:T(8,128)(2,1)} %param.18, f32[8,8,28,128]{3,2,1,0:T(8,128)S(1)} %bitcast.26, f32[64,3584]{1,0:T(8,128)} %get-tuple-element.5, f32[64,3584]{1,0:T(8,128)} %get-tuple-element.6, f32[3584]{0:T(1024)S(1)} %dynamic-slice_subtract_fusion), kind=kOutput, calls=%fused_computation.13 | convolution fusion | flops 471597056 | bytes 10369024 | tf_op jit(solution)/shard_map/dot_general | solution.py:44
  128.5 0.0 reduce-scatter.2.cloned.1.call-update
  128.5 0.4 fusion.20
  128.9 0.4 fusion.4
  129.3 40.1 %all_gather.3 = bf16[64,512]{0,1:T(8,128)(2,1)S(1)} all-gather(bf16[64,16]{0,1:T(8,128)(2,1)S(1)} %fusion.4), channel_id=1, replica_groups=mesh['hot'=8,'cold'=4] {'hot','cold'}, dimensions={1}, use_global_device_ids=true | all-gather | bytes 67584 | tf_op jit(solution)/shard_map/all_gather | solution.py:46
  169.4 0.0 all-to-all-done
  169.4 1.7 fusion.3
  (9 shorter events, 0.0 us)
Async XLA Ops:
  6.5 122.0 %copy-start = (bf16[16,8192]{1,0:T(8,128)(2,1)S(1)}, bf16[16,8192]{1,0:T(8,128)(2,1)}, u32[]{:S(2)}) copy-start(bf16[16,8192]{1,0:T(8,128)(2,1)} %param.12) | copy-start | bytes 786436
  6.5 115.4 %all-reduce.3.cloned.1.call-start = ((), (), s32[]{:S(2)}) async-start(), calls=%async_computation.3 | async-start | bytes 3670016 | tf_op jit(solution)/shard_map/psum | solution.py:42
  8.1 7.3 %slice-start = ((s8[7340032]{0:T(1024)(128)(4,1)}), s8[4194304]{0:T(1024)(128)(4,1)S(1)}, s32[]{:S(2)}) async-start(s8[7340032]{0:T(1024)(128)(4,1)} %bitcast.24), calls=%async_computation.4 | async-start | bytes 8388608
  9.8 5.6 %slice-start.1 = ((s8[7340032]{0:T(1024)(128)(4,1)}), s8[3145728]{0:T(1024)(128)(4,1)S(1)}, s32[]{:S(2)}) async-start(s8[7340032]{0:T(1024)(128)(4,1)} %bitcast.24), calls=%async_computation.5 | async-start | bytes 6291456
  15.4 2.4 %copy-start.2 = (bf16[16,8192]{1,0:T(8,128)(2,1)S(1)}, bf16[16,8192]{1,0:T(8,128)(2,1)}, u32[]{:S(2)}) copy-start(bf16[16,8192]{1,0:T(8,128)(2,1)} %param.14) | copy-start | bytes 786436
  15.4 10.5 %copy-start.3 = (s32[64,28]{0,1:T(8,128)S(1)}, s32[64,28]{0,1:T(8,128)}, u32[]{:S(2)}) copy-start(s32[64,28]{0,1:T(8,128)} %param.19) | copy-start | bytes 21508
  15.5 10.6 %copy-start.4 = (s32[512]{0:T(512)S(1)}, s32[512]{0:T(512)}, u32[]{:S(2)}) copy-start(s32[512]{0:T(512)} %param.15) | copy-start | bytes 6148
  17.8 111.1 %copy-start.1 = (bf16[16,8192]{1,0:T(8,128)(2,1)S(1)}, bf16[16,8192]{1,0:T(8,128)(2,1)}, u32[]{:S(2)}) copy-start(bf16[16,8192]{1,0:T(8,128)(2,1)} %param.13) | copy-start | bytes 786436
  18.5 150.8 %all-to-all-start = ((bf16[16,32,256]{2,0,1:T(8,128)(2,1)}), bf16[16,32,256]{2,0,1:T(8,128)(2,1)S(1)}, u32[]{:S(2)}, u32[]{:S(2)}) async-start(bf16[16,32,256]{2,0,1:T(8,128)(2,1)} %bitcast.23), calls=%async_computation | async-start | bytes 524288 | tf_op jit(solution)/shard_map/all_to_all | solution.py:45
  25.9 143.5 %reduce-scatter.2.cloned.1.call-start = ((), (), s32[]{:S(2)}) async-start(), calls=%async_computation.2 | async-start | bytes 327680 | tf_op jit(solution)/shard_map/reduce_scatter | solution.py:48
Sparse Core Ops, SparseCore 0:
  17.9 103.9 all-reduce.2
  128.6 19.6 reduce-scatter.1
where the time goes:
time: 178 us
  waiting for transfers between devices  93.3 us (52%)
  blocking collectives  40.1 us (23%)
  matrix products  16.5 us (9%)
  between operations  13.5 us (8%)
  starting transfers between devices  7.37 us (4%)
  local copies, waits for them, and re-layouts  3.65 us (2%)
  other arithmetic  3.35 us (2%)
    psum x1, waiting for transfers between devices, on_device(): gate_cold, up_cold = lax.psum((gate_part, up_part), 'hot')  93.3 us
    all_gather x1, blocking collectives, on_device(): hidden_all = lax.all_gather(hidden_hot, ('hot', 'cold'), axis=1, tiled=True)  40.1 us
    all_to_all x1, starting transfers between devices, on_device(): lax.all_to_all(hot_down, ('hot', 'cold'), split_axis=1, concat_axis=0, ti...  7.32 us
    dot_general x1, matrix products, on_device(): out_cold = jnp.dot(hidden_cold, down_w, preferred_element_type=jnp.float32)  6.19 us
    dot_general x1, matrix products, on_device(): up_part = jnp.dot(normed_part, up_w, preferred_element_type=jnp.float32)  5.59 us
  transfers between devices with their start and end apart: 3, of which 1 were waited for; matrix products, arithmetic and copies ran while one was open for 6% of the time, Pallas kernels for 0%

commit v1 on v0

--- a/solution.py
+++ b/solution.py
@@ -4,6 +4,18 @@
 from jax.sharding import PartitionSpec as P
 
 UNITS = 14336
+
+
+def collect(x, axis, dim):
+    ways, here = (lax.axis_size(axis), lax.axis_index(axis))
+    grown, reach = (x, 1)
+    while reach < ways:
+        theirs = lax.ppermute(grown, axis, [(d, d ^ reach) for d in range(ways)])
+        mine_first = jnp.concatenate([grown, theirs], axis=dim)
+        theirs_first = jnp.concatenate([theirs, grown], axis=dim)
+        grown = jnp.where(here & reach == 0, mine_first, theirs_first)
+        reach = 2 * reach
+    return grown
 
 
 def on_device(
@@ -43,7 +55,7 @@
     hidden_cold = (jax.nn.silu(gate_cold) * up_cold * live).astype(jnp.bfloat16)
     out_cold = jnp.dot(hidden_cold, down_w, preferred_element_type=jnp.float32)
     down_cols = lax.all_to_all(hot_down, ("hot", "cold"), split_axis=1, concat_axis=0, tiled=True)
-    hidden_all = lax.all_gather(hidden_hot, ("hot", "cold"), axis=1, tiled=True)
+    hidden_all = collect(hidden_hot, ("hot", "cold"), 1)
     hot_total = jnp.dot(hidden_all, down_cols, preferred_element_type=jnp.float32)
     cold_total = lax.psum_scatter(out_cold, "cold", scatter_dimension=1, tiled=True)
     total = hot_total + cold_total

time: 178 us -> 156 us (0.88)
  blocking collectives: 40.1 us -> 0 us
  waiting for transfers between devices: 93.3 us -> 103 us
  starting transfers between devices: 7.37 us -> 12.7 us
  matrix products: 16.5 us -> 18.7 us
    all_gather x1 -> x0, blocking collectives: 40.1 us -> none  [on_device(): hidden_all = lax.all_gather(hidden_hot, ('hot', 'cold'), axis=1, tiled=True)]
    ppermute x0 -> x5, waiting for transfers between devices: none -> 8.52 us  [collect(): theirs = lax.ppermute(grown, axis, [(d, d ^ reach) for d in range(ways)])]
    ppermute x0 -> x5, starting transfers between devices: none -> 8.48 us  [collect(): theirs = lax.ppermute(grown, axis, [(d, d ^ reach) for d in range(ways)])]
    all_to_all x1, starting transfers between devices: 7.32 us -> 4.17 us  [on_device(): lax.all_to_all(hot_down, ('hot', 'cold'), split_axis=1, concat_axis=0, ti...]
  transfers between devices with their start and end apart: 3 -> 8, of which waited for: 1 -> 5; matrix products, arithmetic and copies ran while one was open for 6% -> 3% of each run, Pallas kernels for 0% -> 0%
where the time goes in v1:
time: 156 us
  waiting for transfers between devices  103 us (66%)
  matrix products  18.7 us (12%)
  between operations  13.6 us (9%)
  starting transfers between devices  12.7 us (8%)
  other arithmetic  4.24 us (3%)
  local copies, waits for them, and re-layouts  3.66 us (2%)
    psum x1, waiting for transfers between devices, on_device(): gate_cold, up_cold = lax.psum((gate_part, up_part), 'hot')  94.4 us
    ppermute x5, waiting for transfers between devices, collect(): theirs = lax.ppermute(grown, axis, [(d, d ^ reach) for d in range(ways)])  8.52 us
    ppermute x5, starting transfers between devices, collect(): theirs = lax.ppermute(grown, axis, [(d, d ^ reach) for d in range(ways)])  8.48 us
    dot_general x1, matrix products, on_device(): out_cold = jnp.dot(hidden_cold, down_w, preferred_element_type=jnp.float32)  6.2 us
    dot_general x1, matrix products, on_device(): up_part = jnp.dot(normed_part, up_w, preferred_element_type=jnp.float32)  5.6 us
    all_to_all x1, starting transfers between devices, on_device(): lax.all_to_all(hot_down, ('hot', 'cold'), split_axis=1, concat_axis=0, ti...  4.17 us
    dot_general x1, matrix products, on_device(): gate_part = jnp.dot(normed_part, gate_w, preferred_element_type=jnp.float32)  3.23 us
  transfers between devices with their start and end apart: 8, of which 5 were waited for; matrix products, arithmetic and copies ran while one was open for 3% of the time, Pallas kernels for 0%

profile of v1, /device:TPU:0, one launch (start us, length us, event | category | flops | bytes accessed | tf_op | source)
XLA Modules:
  0.0 155.8 jit_solution(1884624153393103953)
XLA Ops:
  6.5 1.6 %fusion = f32[64]{0:T(128)S(1)} fusion(bf16[64,8192]{1,0:T(8,128)(2,1)} %param.10), kind=kLoop, calls=%fused_computation.3 | loop fusion | flops 1572800 | bytes 1048832 | tf_op jit(solution)/shard_map/reduce_sum | solution.py:34
  8.1 2.5 %fusion.2 = bf16[64,8192]{1,0:T(8,128)(2,1)} fusion(bf16[64,8192]{1,0:T(8,128)(2,1)} %param.10, f32[8192]{0:T(1024)} %param.11, f32[64]{0:T(128)S(1)} %add_rsqrt_fusion), kind=kLoop, calls=%fused_computation.5 | loop fusion | flops 2097152 | bytes 2130176 | tf_op jit(solution)/shard_map/convert_element_type | solution.py:35
  10.7 5.6 %fusion.17 = f32[64,3584]{1,0:T(8,128)} fusion(bf16[1024,3584]{1,0:T(8,128)(2,1)} %param.17, bf16[64,8192]{1,0:T(8,128)(2,1)} %fusion.2, s32[]{:T(128)S(6)} %select_n.59), kind=kOutput, calls=%fused_computation.24 | convolution fusion | flops 469762048 | bytes 8388612 | tf_op jit(solution)/shard_map/dot_general | solution.py:53
  16.3 0.0 copy-start.5
  16.3 3.2 %fusion.19 = f32[64,3584]{1,0:T(8,128)} fusion(bf16[1024,3584]{1,0:T(8,128)(2,1)S(1)} %bitcast.24, bf16[64,8192]{1,0:T(8,128)(2,1)} %fusion.2, s32[]{:T(128)S(6)} %select_n.59), kind=kOutput, calls=%fused_computation.26 | convolution fusion | flops 469762048 | bytes 8388612 | tf_op jit(solution)/shard_map/dot_general | solution.py:52
  19.5 0.0 all-reduce.3.cloned.1.call-update
  19.5 0.0 copy-start.3
  19.5 0.0 reduce-scatter.2.cloned.1.call-start
  19.6 0.1 copy.16
  19.7 2.5 %scatter_custom_fusion = f32[14336]{0:T(1024)S(1)} fusion(s32[512]{0:T(512)S(1)} %compare_select_fusion, f32[512]{0:T(512)S(1)} %broadcast.20, f32[]{:T(128)} %constant.9.clone.1), kind=kCustom, calls=%fused_computation.30 | custom fusion | bytes 57348 | tf_op jit(solution)/shard_map/scatter | solution.py:45
  22.2 0.1 dynamic-slice_subtract_fusion
  22.3 1.6 %fusion.27 = f32[64,16]{0,1:T(8,128)S(1)} fusion(bf16[64,8192]{1,0:T(8,128)(2,1)} %fusion.2, bf16[16,8192]{1,0:T(8,128)(2,1)S(1)} %copy-done), kind=kOutput, calls=%fused_computation.41 | convolution fusion | flops 16777216 | bytes 1314816 | tf_op jit(solution)/shard_map/dot_general | solution.py:37
  23.9 94.4 %all-reduce.3.cloned.1.call-done = (f32[64,3584]{1,0:T(8,128)}, f32[64,3584]{1,0:T(8,128)}) async-done(((f32[64,3584]{1,0:T(8,128)}, f32[64,3584]{1,0:T(8,128)}), (f32[64,3584]{1,0:T(8,128)}, f32[64,3584]{1,0:T(8,128)})) %all-reduce.3.cloned.1.call-update) | async-done | bytes 1835024 | tf_op jit(solution)/shard_map/psum | solution.py:54
  118.3 0.3 mul.72
  118.6 6.2 %fusion.7 = f32[64,1024]{1,0:T(8,128)} fusion(bf16[3584,1024]{1,0:T(8,128)(2,1)} %param.18, f32[8,8,28,128]{3,2,1,0:T(8,128)S(1)} %bitcast.25, f32[64,3584]{1,0:T(8,128)} %get-tuple-element.5, f32[64,3584]{1,0:T(8,128)} %get-tuple-element.6, f32[3584]{0:T(1024)S(1)} %dynamic-slice_subtract_fusion), kind=kOutput, calls=%fused_computation.13 | convolution fusion | flops 471597056 | bytes 10369024 | tf_op jit(solution)/shard_map/dot_general | solution.py:56
  124.8 0.0 reduce-scatter.2.cloned.1.call-update
  124.9 0.4 fusion.4
  125.2 0.0 collective-permute-start
  125.3 0.0 copy-done.3
  125.3 0.7 copy.22
  126.0 4.2 %all-to-all-start = ((bf16[16,32,256]{2,0,1:T(8,128)(2,1)}), bf16[16,32,256]{2,0,1:T(8,128)(2,1)S(1)}, u32[]{:S(2)}, u32[]{:S(2)}) async-start(bf16[16,32,256]{2,0,1:T(8,128)(2,1)} %bitcast.22), calls=%async_computation | async-start | bytes 524288 | tf_op jit(solution)/shard_map/all_to_all | solution.py:57
  130.2 0.0 collective-permute-done
  130.2 1.8 %collective-permute-start.1 = (bf16[64,32]{0,1:T(8,128)(2,1)S(1)}, bf16[64,32]{0,1:T(8,128)(2,1)S(1)}, u32[]{:S(2)}, u32[]{:S(2)}) collective-permute-start(bf16[64,32]{0,1:T(8,128)(2,1)S(1)} %maximum_select_fusion.5), channel_id=1, source_target_pairs={{0,2},{1,3},{2,0},{3,1},{4,6},{5,7},{6,4},{7,5},{8,10},{9,11},{10,... | collective-permute-start | bytes 12296 | tf_op jit(solution)/shard_map/ppermute | solution.py:13
  132.0 2.0 %collective-permute-done.1 = bf16[64,32]{0,1:T(8,128)(2,1)S(1)} collective-permute-done((bf16[64,32]{0,1:T(8,128)(2,1)S(1)}, bf16[64,32]{0,1:T(8,128)(2,1)S(1)}, u32[]{:S(2)}, u32[]{:S(2)}) %collective-permute-start.1) | collective-permute-done | bytes 4128 | tf_op jit(solution)/shard_map/ppermute | solution.py:13
  134.0 1.9 %collective-permute-start.2 = (bf16[64,64]{0,1:T(8,128)(2,1)S(1)}, bf16[64,64]{0,1:T(8,128)(2,1)S(1)}, u32[]{:S(2)}, u32[]{:S(2)}) collective-permute-start(bf16[64,64]{0,1:T(8,128)(2,1)S(1)} %maximum_select_fusion.4), channel_id=1, source_target_pairs={{0,4},{1,5},{2,6},{3,7},{4,0},{5,1},{6,2},{7,3},{8,12},{9,13},{10,... | collective-permute-start | bytes 24584 | tf_op jit(solution)/shard_map/ppermute | solution.py:13
  135.9 2.1 %collective-permute-done.2 = bf16[64,64]{0,1:T(8,128)(2,1)S(1)} collective-permute-done((bf16[64,64]{0,1:T(8,128)(2,1)S(1)}, bf16[64,64]{0,1:T(8,128)(2,1)S(1)}, u32[]{:S(2)}, u32[]{:S(2)}) %collective-permute-start.2) | collective-permute-done | bytes 8224 | tf_op jit(solution)/shard_map/ppermute | solution.py:13
  138.0 1.9 %collective-permute-start.3 = (bf16[64,128]{0,1:T(8,128)(2,1)S(1)}, bf16[64,128]{0,1:T(8,128)(2,1)S(1)}, u32[]{:S(2)}, u32[]{:S(2)}) collective-permute-start(bf16[64,128]{0,1:T(8,128)(2,1)S(1)} %maximum_select_fusion.3), channel_id=1, source_target_pairs={{0,8},{1,9},{2,10},{3,11},{4,12},{5,13},{6,14},{7,15},{8,0},{9,1},... | collective-permute-start | bytes 49160 | tf_op jit(solution)/shard_map/ppermute | solution.py:13
  139.9 2.1 %collective-permute-done.3 = bf16[64,128]{0,1:T(8,128)(2,1)S(1)} collective-permute-done((bf16[64,128]{0,1:T(8,128)(2,1)S(1)}, bf16[64,128]{0,1:T(8,128)(2,1)S(1)}, u32[]{:S(2)}, u32[]{:S(2)}) %collective-permute-start.3) | collective-permute-done | bytes 16416 | tf_op jit(solution)/shard_map/ppermute | solution.py:13
  142.0 2.9 %collective-permute-start.4 = (bf16[64,256]{0,1:T(8,128)(2,1)S(1)}, bf16[64,256]{0,1:T(8,128)(2,1)S(1)}, u32[]{:S(2)}, u32[]{:S(2)}) collective-permute-start(bf16[64,256]{0,1:T(8,128)(2,1)S(1)} %maximum_select_fusion.2), channel_id=1, source_target_pairs={{0,16},{1,17},{2,18},{3,19},{4,20},{5,21},{6,22},{7,23},{8,24},{9,... | collective-permute-start | bytes 98312 | tf_op jit(solution)/shard_map/ppermute | solution.py:13
  145.0 2.3 %collective-permute-done.4 = bf16[64,256]{0,1:T(8,128)(2,1)S(1)} collective-permute-done((bf16[64,256]{0,1:T(8,128)(2,1)S(1)}, bf16[64,256]{0,1:T(8,128)(2,1)S(1)}, u32[]{:S(2)}, u32[]{:S(2)}) %collective-permute-start.4) | collective-permute-done | bytes 32800 | tf_op jit(solution)/shard_map/ppermute | solution.py:13
  147.3 0.0 all-to-all-done
  147.3 1.7 %fusion.3 = bf16[64,256]{1,0:T(8,128)(2,1)} fusion(f32[64,256]{1,0:T(8,128)} %reduce-scatter.2.cloned.1.call-done, bf16[512,256]{1,0:T(8,128)(2,1)S(1)} %bitcast.27, bf16[64,256]{0,1:T(8,128)(2,1)S(1)} %collective-permute-done.4, bf16[64,256]{0,1:T(8,128)(2,1)S(1)} %maximum_select_fusion.2, pred[]{:T(512)S(6)} %eq.15), kind=kOutput, calls=%fused_computation.7 | convolution fusion | flops 17104896 | bytes 425985 | tf_op jit(solution)/shard_map/dot_general | solution.py:59
  (24 shorter events, 0.1 us)
Async XLA Ops:
  6.5 15.8 %copy-start = (bf16[16,8192]{1,0:T(8,128)(2,1)S(1)}, bf16[16,8192]{1,0:T(8,128)(2,1)}, u32[]{:S(2)}) copy-start(bf16[16,8192]{1,0:T(8,128)(2,1)} %param.12) | copy-start | bytes 786436
  6.5 111.8 %all-reduce.3.cloned.1.call-start = ((), (), s32[]{:S(2)}) async-start(), calls=%async_computation.3 | async-start | bytes 3670016 | tf_op jit(solution)/shard_map/psum | solution.py:54
  10.7 5.6 %slice-start = ((s8[7340032]{0:T(1024)(128)(4,1)}), s8[3145728]{0:T(1024)(128)(4,1)S(1)}, s32[]{:S(2)}) async-start(s8[7340032]{0:T(1024)(128)(4,1)} %bitcast.23), calls=%async_computation.4 | async-start | bytes 6291456
  10.7 5.6 %slice-start.1 = ((s8[7340032]{0:T(1024)(128)(4,1)}), s8[4194304]{0:T(1024)(128)(4,1)S(1)}, s32[]{:S(2)}) async-start(s8[7340032]{0:T(1024)(128)(4,1)} %bitcast.23), calls=%async_computation.5 | async-start | bytes 8388608
  16.3 3.3 %copy-start.4 = (s32[64,28]{0,1:T(8,128)S(1)}, s32[64,28]{0,1:T(8,128)}, u32[]{:S(2)}) copy-start(s32[64,28]{0,1:T(8,128)} %param.19) | copy-start | bytes 21508
  16.3 3.5 %copy-start.5 = (s32[512]{0:T(512)S(1)}, s32[512]{0:T(512)}, u32[]{:S(2)}) copy-start(s32[512]{0:T(512)} %param.15) | copy-start | bytes 6148
  19.5 105.3 %copy-start.1 = (bf16[64,8192]{1,0:T(8,128)(2,1)S(1)}, bf16[64,8192]{1,0:T(8,128)(2,1)}, u32[]{:S(2)}) copy-start(bf16[64,8192]{1,0:T(8,128)(2,1)} %fusion.2) | copy-start | bytes 3145732
  19.5 105.3 %copy-start.2 = (bf16[16,8192]{1,0:T(8,128)(2,1)S(1)}, bf16[16,8192]{1,0:T(8,128)(2,1)}, u32[]{:S(2)}) copy-start(bf16[16,8192]{1,0:T(8,128)(2,1)} %param.13) | copy-start | bytes 786436
  19.5 105.7 %copy-start.3 = (bf16[16,8192]{1,0:T(8,128)(2,1)S(1)}, bf16[16,8192]{1,0:T(8,128)(2,1)}, u32[]{:S(2)}) copy-start(bf16[16,8192]{1,0:T(8,128)(2,1)} %param.14) | copy-start | bytes 786436
  19.5 127.7 %reduce-scatter.2.cloned.1.call-start = ((), (), s32[]{:S(2)}) async-start(), calls=%async_computation.2 | async-start | bytes 327680 | tf_op jit(solution)/shard_map/reduce_scatter | solution.py:60
  125.2 4.9 %collective-permute-start = (bf16[64,16]{0,1:T(8,128)(2,1)S(1)}, bf16[64,16]{0,1:T(8,128)(2,1)S(1)}, u32[]{:S(2)}, u32[]{:S(2)}) collective-permute-start(bf16[64,16]{0,1:T(8,128)(2,1)S(1)} %fusion.4), channel_id=1, source_target_pairs={{0,1},{1,0},{2,3},{3,2},{4,5},{5,4},{6,7},{7,6},{8,9},{9,8},{10,11... | collective-permute-start | bytes 6152 | tf_op jit(solution)/shard_map/ppermute | solution.py:13
  126.0 21.3 %all-to-all-start = ((bf16[16,32,256]{2,0,1:T(8,128)(2,1)}), bf16[16,32,256]{2,0,1:T(8,128)(2,1)S(1)}, u32[]{:S(2)}, u32[]{:S(2)}) async-start(bf16[16,32,256]{2,0,1:T(8,128)(2,1)} %bitcast.22), calls=%async_computation | async-start | bytes 524288 | tf_op jit(solution)/shard_map/all_to_all | solution.py:57
  130.2 3.8 %collective-permute-start.1 = (bf16[64,32]{0,1:T(8,128)(2,1)S(1)}, bf16[64,32]{0,1:T(8,128)(2,1)S(1)}, u32[]{:S(2)}, u32[]{:S(2)}) collective-permute-start(bf16[64,32]{0,1:T(8,128)(2,1)S(1)} %maximum_select_fusion.5), channel_id=1, source_target_pairs={{0,2},{1,3},{2,0},{3,1},{4,6},{5,7},{6,4},{7,5},{8,10},{9,11},{10,... | collective-permute-start | bytes 12296 | tf_op jit(solution)/shard_map/ppermute | solution.py:13
  134.0 4.0 %collective-permute-start.2 = (bf16[64,64]{0,1:T(8,128)(2,1)S(1)}, bf16[64,64]{0,1:T(8,128)(2,1)S(1)}, u32[]{:S(2)}, u32[]{:S(2)}) collective-permute-start(bf16[64,64]{0,1:T(8,128)(2,1)S(1)} %maximum_select_fusion.4), channel_id=1, source_target_pairs={{0,4},{1,5},{2,6},{3,7},{4,0},{5,1},{6,2},{7,3},{8,12},{9,13},{10,... | collective-permute-start | bytes 24584 | tf_op jit(solution)/shard_map/ppermute | solution.py:13
  138.0 4.0 %collective-permute-start.3 = (bf16[64,128]{0,1:T(8,128)(2,1)S(1)}, bf16[64,128]{0,1:T(8,128)(2,1)S(1)}, u32[]{:S(2)}, u32[]{:S(2)}) collective-permute-start(bf16[64,128]{0,1:T(8,128)(2,1)S(1)} %maximum_select_fusion.3), channel_id=1, source_target_pairs={{0,8},{1,9},{2,10},{3,11},{4,12},{5,13},{6,14},{7,15},{8,0},{9,1},... | collective-permute-start | bytes 49160 | tf_op jit(solution)/shard_map/ppermute | solution.py:13
  142.0 5.2 %collective-permute-start.4 = (bf16[64,256]{0,1:T(8,128)(2,1)S(1)}, bf16[64,256]{0,1:T(8,128)(2,1)S(1)}, u32[]{:S(2)}, u32[]{:S(2)}) collective-permute-start(bf16[64,256]{0,1:T(8,128)(2,1)S(1)} %maximum_select_fusion.2), channel_id=1, source_target_pairs={{0,16},{1,17},{2,18},{3,19},{4,20},{5,21},{6,22},{7,23},{8,24},{9,... | collective-permute-start | bytes 98312 | tf_op jit(solution)/shard_map/ppermute | solution.py:13
Sparse Core Ops, SparseCore 0:
  19.7 98.5 all-reduce.2
  125.0 19.5 reduce-scatter.1
